TPU v7x, 32 devices: a whole 2x2x4 slice. The times are simulated.
32 devices in a mesh: dp: 2 (over x), tp: 16 (over y, z, core).
Axes of the slice: x: 2, y: 2, z: 4, core: 2. Of those that a mesh axis runs over, the one named last changes fastest.
Arguments:
- x: bfloat16 [8192, 4096], P(('dp', 'tp')), parts along dimension 0
- dy: bfloat16 [8192, 4096], P(('dp', 'tp')), parts along dimension 0
- gate: bfloat16 [8192, 14336], P('dp', 'tp'), parts along dimension 0
- up: bfloat16 [8192, 14336], P('dp', 'tp'), parts along dimension 0
- w_gate: bfloat16 [4096, 14336], P(None, 'tp')
- w_up: bfloat16 [4096, 14336], P(None, 'tp')
- w_down: bfloat16 [14336, 4096], P('tp')
Outputs:
- output 1: bfloat16 [8192, 4096], P(('dp', 'tp')), parts along dimension 0
- output 2: bfloat16 [8192, 14336], P('dp', 'tp'), parts along dimension 0
- output 3: bfloat16 [8192, 14336], P('dp', 'tp'), parts along dimension 0
- output 4: bfloat16 [28672, 4096], P(('dp', 'tp')), parts along dimension 0
There are 2 independent parts. A program takes and returns all parts, laid end to end along the dimension named above; an argument that names none is the same for every part.
All inputs are finite; a program needn't handle non-finite values.
Results may differ from a plain program's by a relative error of at most 0.012.
Values are sent between devices in bfloat16 or wider.
A program may use at most 2 GiB of HBM per device.

v0:
```python
import jax
import jax.numpy as jnp


def act(gate, up):
    return jax.nn.silu(gate) * up


def solution(mesh):
    def step(x, dy, gate, up, w_gate, w_up, w_down):
        hidden, back = jax.vjp(act, gate.astype(jnp.float32), up.astype(jnp.float32))
        d_hidden = jnp.dot(dy, w_down.T, preferred_element_type=jnp.float32)
        d_gate, d_up = (g.astype(jnp.bfloat16) for g in back(d_hidden))
        dx = jnp.dot(d_gate, w_gate.T) + jnp.dot(d_up, w_up.T)
        groups = mesh.shape["dp"]

        def by_group(a, b):
            a, b = (t.reshape(groups, -1, t.shape[-1]) for t in (a, b))
            product = jnp.einsum("gta,gtb->gab", a, b, preferred_element_type=jnp.float32)
            return product.astype(jnp.bfloat16).reshape(-1, b.shape[-1])

        return dx, by_group(x, d_gate), by_group(x, d_up), by_group(hidden.astype(jnp.bfloat16), dy)

    return step
```

profile of v0, /device:TPU:0, one launch (start us, length us, event | category | flops | bytes accessed | tf_op | source)
XLA Modules:
  0.0 1034.3 jit_solution(5394492899176503282)
XLA Ops:
  11.2 170.0 %all-gather.9.cloned.1.call-done = bf16[4096,4096]{1,0:T(8,128)(2,1)} async-done(((bf16[256,4096]{1,0:T(8,128)(2,1)}), bf16[4096,4096]{1,0:T(8,128)(2,1)}) %all-gather.9.cloned.1.call-update) | async-done | bytes 33554448 | tf_op args[1]
  181.2 42.7 %fusion.23 = f32[4096,896]{1,0:T(8,128)} fusion(bf16[4096,4096]{1,0:T(8,128)(2,1)} %all-gather.9.cloned.1.call-done, bf16[896,4096]{1,0:T(8,128)(2,1)} %param.3), kind=kOutput, calls=%fused_computation.40 | convolution fusion | flops 30064771072 | bytes 55574528 | tf_op jit(solution)/dot_general | solution.py:12
  223.9 16.9 %fusion.22 = (bf16[1,4096,896]{2,1,0:T(8,128)(2,1)}, bf16[4096,896]{1,0:T(8,128)(2,1)}) fusion(bf16[4096,896]{1,0:T(8,128)(2,1)} %param.4, bf16[4096,896]{1,0:T(8,128)(2,1)} %param.5, f32[4096,896]{1,0:T(8,128)} %fusion.23), kind=kLoop, calls=%fused_computation.36 | loop fusion | flops 58720256 | bytes 44040192 | tf_op jit(solution)/reshape | solution.py:18
  240.8 42.8 %fusion.24 = bf16[4096,4096]{1,0:T(8,128)(2,1)} fusion(bf16[4096,896]{1,0:T(8,128)(2,1)} %get-tuple-element.45, bf16[4096,896]{1,0:T(8,128)(2,1)} %param.6), kind=kOutput, calls=%fused_computation.41 | convolution fusion | flops 30064771072 | bytes 48234496 | tf_op jit(solution)/dot_general | solution.py:14
  283.6 44.4 %convolution_add_fusion = bf16[4096,4096]{1,0:T(8,128)(2,1)} fusion(bf16[4096,4096]{1,0:T(8,128)(2,1)} %fusion.24, bf16[4096,896]{1,0:T(8,128)(2,1)} %param.7, f32[4096,896]{1,0:T(8,128)} %fusion.23, bf16[4096,896]{1,0:T(8,128)(2,1)} %param.5), kind=kOutput, calls=%fused_computation.21 | convolution fusion | flops 30107238400 | bytes 96468992 | tf_op jit(solution)/dot_general | solution.py:14
  328.3 30.1 %all-gather.11.cloned.1.call-done = bf16[4096,4096]{1,0:T(8,128)(2,1)} async-done(((bf16[256,4096]{1,0:T(8,128)(2,1)}), bf16[4096,4096]{1,0:T(8,128)(2,1)}) %all-gather.11.cloned.1.call-update) | async-done | bytes 33554448 | tf_op jit(solution)/reshape | solution.py:18
  358.4 38.4 %convert_bitcast_fusion.1 = bf16[4096,896]{0,1:T(8,128)(2,1)} fusion(bf16[4096,896]{1,0:T(8,128)(2,1)} %get-tuple-element.45, bf16[4096,4096]{1,0:T(8,128)(2,1)} %all-gather.11.cloned.1.call-done), kind=kOutput, calls=%fused_computation.38 | convolution fusion | flops 30068441088 | bytes 48234496 | tf_op jit(solution)/gta,gtb->gab/dot_general | solution.py:19
  396.8 10.8 %copy.1 = bf16[4096,896]{1,0:T(8,128)(2,1)} copy(bf16[4096,896]{0,1:T(8,128)(2,1)} %convert_bitcast_fusion.1) | data formatting | bytes 14680064
  407.6 47.3 %convert_bitcast_fusion = bf16[4096,896]{0,1:T(8,128)(2,1)} fusion(bf16[4096,4096]{1,0:T(8,128)(2,1)} %all-gather.11.cloned.1.call-done, f32[4096,896]{1,0:T(8,128)} %fusion.23, bf16[4096,896]{1,0:T(8,128)(2,1)} %param.5), kind=kOutput, calls=%fused_computation.37 | convolution fusion | flops 30094131200 | bytes 62914560 | tf_op jit(solution)/gta,gtb->gab/dot_general | solution.py:19
  454.8 10.8 %copy.2 = bf16[4096,896]{1,0:T(8,128)(2,1)} copy(bf16[4096,896]{0,1:T(8,128)(2,1)} %convert_bitcast_fusion) | data formatting | bytes 14680064
  465.7 10.7 %copy = bf16[1,4096,896]{1,2,0:T(8,128)(2,1)} copy(bf16[1,4096,896]{2,1,0:T(8,128)(2,1)} %get-tuple-element.44) | data formatting | bytes 14680064
  476.4 541.5 %while.2 = (bf16[1,4096,896]{1,2,0:T(8,128)(2,1)}, bf16[1,1,256,4096]{3,2,1,0:T(8,128)(2,1)}, f32[1,896,4096]{2,1,0:T(8,128)}, bf16[1,1,256,4096]{3,2,1,0:T(8,12...) while((bf16[1,4096,896]{1,2,0:T(8,128)(2,1)}, ...), condition=%wide.windowed_dot_general_cond_ag.clone, body=%wide.windowed_dot_general_body_ag.clone.sunk | while | flops 7535067136 | bytes 123732528 | solution.py:19
  488.5 85.2 %collective-permute-done = bf16[1,1,256,4096]{3,2,1,0:T(8,128)(2,1)} collective-permute-done((bf16[1,1,256,4096]{3,2,1,0:T(8,128)(2,1)S(1)}, bf16[1,1,256,4096]{3,2,1,0:T(8,128)(2,1)}, u32[]{:S(2)}, u32[]{:S(2)}) %collective-permute-start) | collective-permute-done | bytes 2097184 | tf_op jit(solution)/gta,gtb->gab/dot_general | solution.py:19
  580.4 20.4 %collective-permute-start.3 = (bf16[1,1,256,4096]{3,2,1,0:T(8,128)(2,1)}, bf16[1,1,256,4096]{3,2,1,0:T(8,128)(2,1)}, u32[]{:S(2)}, u32[]{:S(2)}) collective-permute-start(bf16[1,1,256,4096]{3,2,1,0:T(8,128)(2,1)} %collective-permute-done.2), channel_id=13, source_target_pairs={{0,1},{1,2},{2,3},{3,4},{4,5},{5,6},{6,7},{7,8},{8,9},{9,10},{10,1... | collective-permute-start | bytes 6291464 | tf_op jit(solution)/gta,gtb->gab/dot_general | solution.py:19
  600.8 11.1 %fusion.39 = f32[896,4096,1]{1,0,2:T(8,128)} fusion(bf16[1,1,256,4096]{3,2,1,0:T(8,128)(2,1)} %copy.9, bf16[1,1,256,4096]{3,2,1,0:T(8,128)(2,1)S(1)} %copy.7, s32[]{:T(128)S(6)} %multiply.15, bf16[1,1,4096,896]{2,3,1,0:T(8,128)(2,1)} %bitcast.65, s32[]{:T(128)S(6)} %multiply.16), kind=kOutput, calls=%fused_computation.7.clone.1 | convolution fusion | flops 3762028544 | bytes 26214408 | tf_op jit(solution)/gta,gtb->gab/dot_general | solution.py:19
  611.9 11.7 %bitcast_add_fusion.3 = f32[1,896,4096]{2,1,0:T(8,128)} fusion(f32[896,4096,1]{1,0,2:T(8,128)} %fusion.39, f32[1,896,4096]{2,1,0:T(8,128)} %get-tuple-element.90, pred[]{:T(512)S(6)} %compare.6, bf16[1,1,256,4096]{3,2,1,0:T(8,128)(2,1)} %collective-permute-done.2, bf16[1,1,256,4096]{3,2,1,0:T(8,128)(2,1)} %collective-permute-done, s32[]{:T(128)S(6)} %multiply.17, ...), kind=kOutput, calls=%fused_computation.4.clone.1 | convolution fusion | flops 3773038592 | bytes 55574536 | tf_op jit(solution)/gta,gtb->gab/dot_general | solution.py:19
  623.6 15.9 %collective-permute-done.1 = bf16[1,1,256,4096]{3,2,1,0:T(8,128)(2,1)} collective-permute-done((bf16[1,1,256,4096]{3,2,1,0:T(8,128)(2,1)}, bf16[1,1,256,4096]{3,2,1,0:T(8,128)(2,1)}, u32[]{:S(2)}, u32[]{:S(2)}) %collective-permute-start.1) | collective-permute-done | bytes 2097184 | tf_op jit(solution)/gta,gtb->gab/dot_general | solution.py:19
  639.6 12.8 %collective-permute-done.3 = bf16[1,1,256,4096]{3,2,1,0:T(8,128)(2,1)} collective-permute-done((bf16[1,1,256,4096]{3,2,1,0:T(8,128)(2,1)}, bf16[1,1,256,4096]{3,2,1,0:T(8,128)(2,1)}, u32[]{:S(2)}, u32[]{:S(2)}) %collective-permute-start.3) | collective-permute-done | bytes 2097184 | tf_op jit(solution)/gta,gtb->gab/dot_general | solution.py:19
  660.1 36.9 %collective-permute-done = bf16[1,1,256,4096]{3,2,1,0:T(8,128)(2,1)} collective-permute-done((bf16[1,1,256,4096]{3,2,1,0:T(8,128)(2,1)S(1)}, bf16[1,1,256,4096]{3,2,1,0:T(8,128)(2,1)}, u32[]{:S(2)}, u32[]{:S(2)}) %collective-permute-start) | collective-permute-done | bytes 2097184 | tf_op jit(solution)/gta,gtb->gab/dot_general | solution.py:19
  704.3 11.1 %fusion.39 = f32[896,4096,1]{1,0,2:T(8,128)} fusion(bf16[1,1,256,4096]{3,2,1,0:T(8,128)(2,1)} %copy.9, bf16[1,1,256,4096]{3,2,1,0:T(8,128)(2,1)S(1)} %copy.7, s32[]{:T(128)S(6)} %multiply.15, bf16[1,1,4096,896]{2,3,1,0:T(8,128)(2,1)} %bitcast.65, s32[]{:T(128)S(6)} %multiply.16), kind=kOutput, calls=%fused_computation.7.clone.1 | convolution fusion | flops 3762028544 | bytes 26214408 | tf_op jit(solution)/gta,gtb->gab/dot_general | solution.py:19
  715.4 18.6 %bitcast_add_fusion.3 = f32[1,896,4096]{2,1,0:T(8,128)} fusion(f32[896,4096,1]{1,0,2:T(8,128)} %fusion.39, f32[1,896,4096]{2,1,0:T(8,128)} %get-tuple-element.90, pred[]{:T(512)S(6)} %compare.6, bf16[1,1,256,4096]{3,2,1,0:T(8,128)(2,1)} %collective-permute-done.2, bf16[1,1,256,4096]{3,2,1,0:T(8,128)(2,1)} %collective-permute-done, s32[]{:T(128)S(6)} %multiply.17, ...), kind=kOutput, calls=%fused_computation.4.clone.1 | convolution fusion | flops 3773038592 | bytes 55574536 | tf_op jit(solution)/gta,gtb->gab/dot_general | solution.py:19
  733.9 49.3 %collective-permute-done.1 = bf16[1,1,256,4096]{3,2,1,0:T(8,128)(2,1)} collective-permute-done((bf16[1,1,256,4096]{3,2,1,0:T(8,128)(2,1)}, bf16[1,1,256,4096]{3,2,1,0:T(8,128)(2,1)}, u32[]{:S(2)}, u32[]{:S(2)}) %collective-permute-start.1) | collective-permute-done | bytes 2097184 | tf_op jit(solution)/gta,gtb->gab/dot_general | solution.py:19
  795.1 63.6 %collective-permute-done = bf16[1,1,256,4096]{3,2,1,0:T(8,128)(2,1)} collective-permute-done((bf16[1,1,256,4096]{3,2,1,0:T(8,128)(2,1)S(1)}, bf16[1,1,256,4096]{3,2,1,0:T(8,128)(2,1)}, u32[]{:S(2)}, u32[]{:S(2)}) %collective-permute-start) | collective-permute-done | bytes 2097184 | tf_op jit(solution)/gta,gtb->gab/dot_general | solution.py:19
  863.4 13.4 %collective-permute-done.2 = bf16[1,1,256,4096]{3,2,1,0:T(8,128)(2,1)} collective-permute-done((bf16[1,1,256,4096]{3,2,1,0:T(8,128)(2,1)}, bf16[1,1,256,4096]{3,2,1,0:T(8,128)(2,1)}, u32[]{:S(2)}, u32[]{:S(2)}) %collective-permute-start.2) | collective-permute-done | bytes 2097184 | tf_op jit(solution)/gta,gtb->gab/dot_general | solution.py:19
  876.8 11.1 %fusion.39 = f32[896,4096,1]{1,0,2:T(8,128)} fusion(bf16[1,1,256,4096]{3,2,1,0:T(8,128)(2,1)} %copy.9, bf16[1,1,256,4096]{3,2,1,0:T(8,128)(2,1)S(1)} %copy.7, s32[]{:T(128)S(6)} %multiply.15, bf16[1,1,4096,896]{2,3,1,0:T(8,128)(2,1)} %bitcast.65, s32[]{:T(128)S(6)} %multiply.16), kind=kOutput, calls=%fused_computation.7.clone.1 | convolution fusion | flops 3762028544 | bytes 26214408 | tf_op jit(solution)/gta,gtb->gab/dot_general | solution.py:19
  887.8 18.6 %bitcast_add_fusion.3 = f32[1,896,4096]{2,1,0:T(8,128)} fusion(f32[896,4096,1]{1,0,2:T(8,128)} %fusion.39, f32[1,896,4096]{2,1,0:T(8,128)} %get-tuple-element.90, pred[]{:T(512)S(6)} %compare.6, bf16[1,1,256,4096]{3,2,1,0:T(8,128)(2,1)} %collective-permute-done.2, bf16[1,1,256,4096]{3,2,1,0:T(8,128)(2,1)} %collective-permute-done, s32[]{:T(128)S(6)} %multiply.17, ...), kind=kOutput, calls=%fused_computation.4.clone.1 | convolution fusion | flops 3773038592 | bytes 55574536 | tf_op jit(solution)/gta,gtb->gab/dot_general | solution.py:19
  907.9 14.9 %collective-permute-done.3 = bf16[1,1,256,4096]{3,2,1,0:T(8,128)(2,1)} collective-permute-done((bf16[1,1,256,4096]{3,2,1,0:T(8,128)(2,1)}, bf16[1,1,256,4096]{3,2,1,0:T(8,128)(2,1)}, u32[]{:S(2)}, u32[]{:S(2)}) %collective-permute-start.3) | collective-permute-done | bytes 2097184 | tf_op jit(solution)/gta,gtb->gab/dot_general | solution.py:19
  930.6 36.9 %collective-permute-done = bf16[1,1,256,4096]{3,2,1,0:T(8,128)(2,1)} collective-permute-done((bf16[1,1,256,4096]{3,2,1,0:T(8,128)(2,1)S(1)}, bf16[1,1,256,4096]{3,2,1,0:T(8,128)(2,1)}, u32[]{:S(2)}, u32[]{:S(2)}) %collective-permute-start) | collective-permute-done | bytes 2097184 | tf_op jit(solution)/gta,gtb->gab/dot_general | solution.py:19
  974.8 11.1 %fusion.39 = f32[896,4096,1]{1,0,2:T(8,128)} fusion(bf16[1,1,256,4096]{3,2,1,0:T(8,128)(2,1)} %copy.9, bf16[1,1,256,4096]{3,2,1,0:T(8,128)(2,1)S(1)} %copy.7, s32[]{:T(128)S(6)} %multiply.15, bf16[1,1,4096,896]{2,3,1,0:T(8,128)(2,1)} %bitcast.65, s32[]{:T(128)S(6)} %multiply.16), kind=kOutput, calls=%fused_computation.7.clone.1 | convolution fusion | flops 3762028544 | bytes 26214408 | tf_op jit(solution)/gta,gtb->gab/dot_general | solution.py:19
  985.9 18.6 %bitcast_add_fusion.3 = f32[1,896,4096]{2,1,0:T(8,128)} fusion(f32[896,4096,1]{1,0,2:T(8,128)} %fusion.39, f32[1,896,4096]{2,1,0:T(8,128)} %get-tuple-element.90, pred[]{:T(512)S(6)} %compare.6, bf16[1,1,256,4096]{3,2,1,0:T(8,128)(2,1)} %collective-permute-done.2, bf16[1,1,256,4096]{3,2,1,0:T(8,128)(2,1)} %collective-permute-done, s32[]{:T(128)S(6)} %multiply.17, ...), kind=kOutput, calls=%fused_computation.4.clone.1 | convolution fusion | flops 3773038592 | bytes 55574536 | tf_op jit(solution)/gta,gtb->gab/dot_general | solution.py:19
  1004.5 13.4 %collective-permute-done.1 = bf16[1,1,256,4096]{3,2,1,0:T(8,128)(2,1)} collective-permute-done((bf16[1,1,256,4096]{3,2,1,0:T(8,128)(2,1)}, bf16[1,1,256,4096]{3,2,1,0:T(8,128)(2,1)}, u32[]{:S(2)}, u32[]{:S(2)}) %collective-permute-start.1) | collective-permute-done | bytes 2097184 | tf_op jit(solution)/gta,gtb->gab/dot_general | solution.py:19
  1017.9 9.4 convert_bitcast_fusion.2
  (46 shorter events, 63.4 us)
Async XLA Ops:
  7.2 174.1 %all-gather.9.cloned.1.call-start = ((), (), s32[]{:S(2)}) async-start(), calls=%async_computation.1 | async-start | bytes 35651584 | tf_op args[1]
  10.4 348.0 %all-gather.11.cloned.1.call-start = ((), (), s32[]{:S(2)}) async-start(), calls=%async_computation.2 | async-start | bytes 35651584 | tf_op jit(solution)/reshape | solution.py:18
  11.1 1016.1 %reduce-scatter.4.cloned.1.call-start = ((), (), s32[]{:S(2)}) async-start(), calls=%async_computation.3 | async-start | bytes 35651584
  328.0 148.4 %collective-permute-start.4 = (bf16[1,1,256,4096]{3,2,1,0:T(8,128)(2,1)}, bf16[1,1,256,4096]{3,2,1,0:T(8,128)(2,1)}, u32[]{:S(2)}, u32[]{:S(2)}) collective-permute-start(bf16[1,1,256,4096]{3,2,1,0:T(8,128)(2,1)} %bitcast.8), channel_id=9, source_target_pairs={{0,1},{1,2},{2,3},{3,4},{4,5},{5,6},{6,7},{7,8},{8,9},{9,10},{10,1... | collective-permute-start | bytes 6291464 | tf_op jit(solution)/gta,gtb->gab/dot_general | solution.py:19
  465.7 10.7 %copy-start = (u32[32]{0:T(128)S(1)}, u32[32]{0:T(128)}, u32[]{:S(2)}) copy-start(u32[32]{0:T(128)} %constant.146) | copy-start | bytes 388
  478.3 95.5 %collective-permute-start = (bf16[1,1,256,4096]{3,2,1,0:T(8,128)(2,1)S(1)}, bf16[1,1,256,4096]{3,2,1,0:T(8,128)(2,1)}, u32[]{:S(2)}, u32[]{:S(2)}) collective-permute-start(bf16[1,1,256,4096]{3,2,1,0:T(8,128)(2,1)S(1)} %copy.7), channel_id=10, source_target_pairs={{0,15},{1,0},{2,1},{3,2},{4,3},{5,4},{6,5},{7,6},{8,7},{9,8},{10,9... | collective-permute-start | bytes 6291464 | tf_op jit(solution)/gta,gtb->gab/dot_general | solution.py:19
  486.0 94.4 %collective-permute-start.2 = (bf16[1,1,256,4096]{3,2,1,0:T(8,128)(2,1)}, bf16[1,1,256,4096]{3,2,1,0:T(8,128)(2,1)}, u32[]{:S(2)}, u32[]{:S(2)}) collective-permute-start(bf16[1,1,256,4096]{3,2,1,0:T(8,128)(2,1)} %copy.9), channel_id=11, source_target_pairs={{0,1},{1,2},{2,3},{3,4},{4,5},{5,6},{6,7},{7,8},{8,9},{9,10},{10,1... | collective-permute-start | bytes 6291464 | tf_op jit(solution)/gta,gtb->gab/dot_general | solution.py:19
  573.8 65.8 %collective-permute-start.1 = (bf16[1,1,256,4096]{3,2,1,0:T(8,128)(2,1)}, bf16[1,1,256,4096]{3,2,1,0:T(8,128)(2,1)}, u32[]{:S(2)}, u32[]{:S(2)}) collective-permute-start(bf16[1,1,256,4096]{3,2,1,0:T(8,128)(2,1)} %collective-permute-done), channel_id=12, source_target_pairs={{0,15},{1,0},{2,1},{3,2},{4,3},{5,4},{6,5},{7,6},{8,7},{9,8},{10,9... | collective-permute-start | bytes 6291464 | tf_op jit(solution)/gta,gtb->gab/dot_general | solution.py:19
  580.4 71.9 %collective-permute-start.3 = (bf16[1,1,256,4096]{3,2,1,0:T(8,128)(2,1)}, bf16[1,1,256,4096]{3,2,1,0:T(8,128)(2,1)}, u32[]{:S(2)}, u32[]{:S(2)}) collective-permute-start(bf16[1,1,256,4096]{3,2,1,0:T(8,128)(2,1)} %collective-permute-done.2), channel_id=13, source_target_pairs={{0,1},{1,2},{2,3},{3,4},{4,5},{5,6},{6,7},{7,8},{8,9},{9,10},{10,1... | collective-permute-start | bytes 6291464 | tf_op jit(solution)/gta,gtb->gab/dot_general | solution.py:19
  653.9 43.1 %collective-permute-start = (bf16[1,1,256,4096]{3,2,1,0:T(8,128)(2,1)S(1)}, bf16[1,1,256,4096]{3,2,1,0:T(8,128)(2,1)}, u32[]{:S(2)}, u32[]{:S(2)}) collective-permute-start(bf16[1,1,256,4096]{3,2,1,0:T(8,128)(2,1)S(1)} %copy.7), channel_id=10, source_target_pairs={{0,15},{1,0},{2,1},{3,2},{4,3},{5,4},{6,5},{7,6},{8,7},{9,8},{10,9... | collective-permute-start | bytes 6291464 | tf_op jit(solution)/gta,gtb->gab/dot_general | solution.py:19
  657.0 47.3 %collective-permute-start.2 = (bf16[1,1,256,4096]{3,2,1,0:T(8,128)(2,1)}, bf16[1,1,256,4096]{3,2,1,0:T(8,128)(2,1)}, u32[]{:S(2)}, u32[]{:S(2)}) collective-permute-start(bf16[1,1,256,4096]{3,2,1,0:T(8,128)(2,1)} %copy.9), channel_id=11, source_target_pairs={{0,1},{1,2},{2,3},{3,4},{4,5},{5,6},{6,7},{7,8},{8,9},{9,10},{10,1... | collective-permute-start | bytes 6291464 | tf_op jit(solution)/gta,gtb->gab/dot_general | solution.py:19
  697.0 86.2 %collective-permute-start.1 = (bf16[1,1,256,4096]{3,2,1,0:T(8,128)(2,1)}, bf16[1,1,256,4096]{3,2,1,0:T(8,128)(2,1)}, u32[]{:S(2)}, u32[]{:S(2)}) collective-permute-start(bf16[1,1,256,4096]{3,2,1,0:T(8,128)(2,1)} %collective-permute-done), channel_id=12, source_target_pairs={{0,15},{1,0},{2,1},{3,2},{4,3},{5,4},{6,5},{7,6},{8,7},{9,8},{10,9... | collective-permute-start | bytes 6291464 | tf_op jit(solution)/gta,gtb->gab/dot_general | solution.py:19
  704.3 81.0 %collective-permute-start.3 = (bf16[1,1,256,4096]{3,2,1,0:T(8,128)(2,1)}, bf16[1,1,256,4096]{3,2,1,0:T(8,128)(2,1)}, u32[]{:S(2)}, u32[]{:S(2)}) collective-permute-start(bf16[1,1,256,4096]{3,2,1,0:T(8,128)(2,1)} %collective-permute-done.2), channel_id=13, source_target_pairs={{0,1},{1,2},{2,3},{3,4},{4,5},{5,6},{6,7},{7,8},{8,9},{9,10},{10,1... | collective-permute-start | bytes 6291464 | tf_op jit(solution)/gta,gtb->gab/dot_general | solution.py:19
  786.9 71.8 %collective-permute-start = (bf16[1,1,256,4096]{3,2,1,0:T(8,128)(2,1)S(1)}, bf16[1,1,256,4096]{3,2,1,0:T(8,128)(2,1)}, u32[]{:S(2)}, u32[]{:S(2)}) collective-permute-start(bf16[1,1,256,4096]{3,2,1,0:T(8,128)(2,1)S(1)} %copy.7), channel_id=10, source_target_pairs={{0,15},{1,0},{2,1},{3,2},{4,3},{5,4},{6,5},{7,6},{8,7},{9,8},{10,9... | collective-permute-start | bytes 6291464 | tf_op jit(solution)/gta,gtb->gab/dot_general | solution.py:19
  792.6 84.2 %collective-permute-start.2 = (bf16[1,1,256,4096]{3,2,1,0:T(8,128)(2,1)}, bf16[1,1,256,4096]{3,2,1,0:T(8,128)(2,1)}, u32[]{:S(2)}, u32[]{:S(2)}) collective-permute-start(bf16[1,1,256,4096]{3,2,1,0:T(8,128)(2,1)} %copy.9), channel_id=11, source_target_pairs={{0,1},{1,2},{2,3},{3,4},{4,5},{5,6},{6,7},{7,8},{8,9},{9,10},{10,1... | collective-permute-start | bytes 6291464 | tf_op jit(solution)/gta,gtb->gab/dot_general | solution.py:19
  858.7 49.2 %collective-permute-start.1 = (bf16[1,1,256,4096]{3,2,1,0:T(8,128)(2,1)}, bf16[1,1,256,4096]{3,2,1,0:T(8,128)(2,1)}, u32[]{:S(2)}, u32[]{:S(2)}) collective-permute-start(bf16[1,1,256,4096]{3,2,1,0:T(8,128)(2,1)} %collective-permute-done), channel_id=12, source_target_pairs={{0,15},{1,0},{2,1},{3,2},{4,3},{5,4},{6,5},{7,6},{8,7},{9,8},{10,9... | collective-permute-start | bytes 6291464 | tf_op jit(solution)/gta,gtb->gab/dot_general | solution.py:19
  876.8 46.1 %collective-permute-start.3 = (bf16[1,1,256,4096]{3,2,1,0:T(8,128)(2,1)}, bf16[1,1,256,4096]{3,2,1,0:T(8,128)(2,1)}, u32[]{:S(2)}, u32[]{:S(2)}) collective-permute-start(bf16[1,1,256,4096]{3,2,1,0:T(8,128)(2,1)} %collective-permute-done.2), channel_id=13, source_target_pairs={{0,1},{1,2},{2,3},{3,4},{4,5},{5,6},{6,7},{7,8},{8,9},{9,10},{10,1... | collective-permute-start | bytes 6291464 | tf_op jit(solution)/gta,gtb->gab/dot_general | solution.py:19
  924.4 43.1 %collective-permute-start = (bf16[1,1,256,4096]{3,2,1,0:T(8,128)(2,1)S(1)}, bf16[1,1,256,4096]{3,2,1,0:T(8,128)(2,1)}, u32[]{:S(2)}, u32[]{:S(2)}) collective-permute-start(bf16[1,1,256,4096]{3,2,1,0:T(8,128)(2,1)S(1)} %copy.7), channel_id=10, source_target_pairs={{0,15},{1,0},{2,1},{3,2},{4,3},{5,4},{6,5},{7,6},{8,7},{9,8},{10,9... | collective-permute-start | bytes 6291464 | tf_op jit(solution)/gta,gtb->gab/dot_general | solution.py:19
  927.6 47.3 %collective-permute-start.2 = (bf16[1,1,256,4096]{3,2,1,0:T(8,128)(2,1)}, bf16[1,1,256,4096]{3,2,1,0:T(8,128)(2,1)}, u32[]{:S(2)}, u32[]{:S(2)}) collective-permute-start(bf16[1,1,256,4096]{3,2,1,0:T(8,128)(2,1)} %copy.9), channel_id=11, source_target_pairs={{0,1},{1,2},{2,3},{3,4},{4,5},{5,6},{6,7},{7,8},{8,9},{9,10},{10,1... | collective-permute-start | bytes 6291464 | tf_op jit(solution)/gta,gtb->gab/dot_general | solution.py:19
  967.5 50.4 %collective-permute-start.1 = (bf16[1,1,256,4096]{3,2,1,0:T(8,128)(2,1)}, bf16[1,1,256,4096]{3,2,1,0:T(8,128)(2,1)}, u32[]{:S(2)}, u32[]{:S(2)}) collective-permute-start(bf16[1,1,256,4096]{3,2,1,0:T(8,128)(2,1)} %collective-permute-done), channel_id=12, source_target_pairs={{0,15},{1,0},{2,1},{3,2},{4,3},{5,4},{6,5},{7,6},{8,7},{9,8},{10,9... | collective-permute-start | bytes 6291464 | tf_op jit(solution)/gta,gtb->gab/dot_general | solution.py:19
  974.8 43.1 %collective-permute-start.3 = (bf16[1,1,256,4096]{3,2,1,0:T(8,128)(2,1)}, bf16[1,1,256,4096]{3,2,1,0:T(8,128)(2,1)}, u32[]{:S(2)}, u32[]{:S(2)}) collective-permute-start(bf16[1,1,256,4096]{3,2,1,0:T(8,128)(2,1)} %collective-permute-done.2), channel_id=13, source_target_pairs={{0,1},{1,2},{2,3},{3,4},{4,5},{5,6},{6,7},{7,8},{8,9},{9,10},{10,1... | collective-permute-start | bytes 6291464 | tf_op jit(solution)/gta,gtb->gab/dot_general | solution.py:19
Sparse Core Ops, SparseCore 0:
  10.5 170.6 all-gather.8
  182.8 175.5 all-gather.10
  363.2 476.6 reduce-scatter.3
where the time goes:
time: 1040 us; the launch traced here: 1030 us
  waiting for transfers between devices  554 us (53%)
  matrix products  327 us (31%)
  local copies, waits for them, and re-layouts  56.9 us (5%)
  starting transfers between devices  47.5 us (5%)
  other arithmetic  26.2 us (3%)
  between operations  14.3 us (1%)
    dot_general x17, waiting for transfers between devices, by_group(): jnp.einsum('gta,gtb->gab', a, b, preferred_element_type=jnp.float32)  353 us
    dot_general x10, matrix products, by_group(): jnp.einsum('gta,gtb->gab', a, b, preferred_element_type=jnp.float32)  197 us
    unnamed x5, waiting for transfers between devices  171 us
    dot_general x2, matrix products, step(): dx = jnp.dot(d_gate, w_gate.T) + jnp.dot(d_up, w_up.T)  87.2 us
    dot_general x17, starting transfers between devices, by_group(): jnp.einsum('gta,gtb->gab', a, b, preferred_element_type=jnp.float32)  47.4 us
    dot_general x1, matrix products, step(): d_hidden = jnp.dot(dy, w_down.T, preferred_element_type=jnp.float32)  42.7 us
    unnamed x6, local copies, waits for them, and re-layouts  35.5 us
    reshape x1, waiting for transfers between devices, by_group(): a, b = (t.reshape(groups, -1, t.shape[-1]) for t in (a, b))  30.1 us
  transfers between devices with their start and end apart: 20, of which 17 were waited for; matrix products, arithmetic and copies ran while one was open for 39% of the time, Pallas kernels for 0%

commit v1 on v0

v1 whole, which is shorter than its diff:
```python
import jax
import jax.numpy as jnp
from jax import lax
from jax.experimental import pallas as pl
from jax.experimental.pallas import tpu as pltpu
from jax.sharding import PartitionSpec as P

BF, F32 = jnp.bfloat16, jnp.float32
LIMIT = 67043328
R, D, C = 256, 4096, 896
HB, HN = R // 2, D // 2
NB = 16
W, WP = 512, 256
QA = 12
NT, TT = (((1,), (1,)), ((), ())), (((0,), (0,)), ((), ()))
DY, X = 0, 1

LINKS = {
    "C": {
        "in": "d000d001x000x001",
        "out": "",
        "y": "d000d001d100d101d200d201d300x000x001x100x101x200x201x300x301",
    },
    "M": {
        "in": "d100d101d000d001x100d011x101x000x001",
        "out": "d100d101d200d201d300d301x100d311x101x200x201x300x301",
        "y": "d100d101d000d001d200d201d300x100x101x000x001x200x201x300x301",
    },
}
OWN = {"C": 0, "M": 1}
NONE, T1, T2P, T2O, DWD, P1 = range(6)
TASKS = {
    "C": (
        ("t000t001p001", "", "t100t010t101t011", "p101p011", "t110t111p111o00-o01-", "t200t201p201", "t300t301p301o10-o11-",
         "t210t211p211", "t310t311p311o20-o21-"),
        ("d03-", "o30-o31-d35-", "d58-", "o40-o41-", "x04-", "o50-o51-x48-o60-", "o61-x8c-", "xcg-", "o70-o71-"),
    ),
    "M": (
        ("t100t101p101", "", "t000t200t110t001", "t201t111p001", "t300t010t301t011", "p301p201p111", "t210t211p211p011", "",
         "t310t311p311o00-"),
        ("o01-d02-", "d24-o10-", "o11-d46-", "o20-o30-d68-", "o21-o31-x04-", "o40-o60-x48-o50-", "o41-o61-o51-x8c-", "xcg-", "o70-o71-"),
    ),
}
IN, OUT, Y, HERE = range(4)
SUMS = {
    "C": ("1100I", "3000I", "3100I", "2100I", "2000I", "1000I", "0101Y", "0001H"),
    "M": ("3010I", "3110I", "2110I", "0101O", "2010I", "0001O", "1111Y", "1011H"),
}


def fours(text):
    return [text[n:n + 4] for n in range(0, len(text), 4)]


def parse(token):
    return ("dx".index(token[0]), *map(int, token[1:]))


def services(kind):
    waits, sends = {}, {}
    arrivals = [(s, parse(e)) for s, e in enumerate(fours(LINKS["M" if kind == "C" else "C"]["out" if kind == "C" else "in"]))]
    if kind == "M":
        for s, e in enumerate(fours(LINKS["M"]["in"])):
            a, p, yr, h = parse(e)
            arrivals.append((s, (a, 3 - p, yr, h)))
    for s, e in enumerate(fours(LINKS[kind]["y"])):
        a, p, _, h = parse(e)
        arrivals.append((s, (a, p, 1, h)))
    for s, e in arrivals:
        waits.setdefault(s + 1, []).append(e)
        sends.setdefault(s + 1, []).append((*e, "d2d"))
    for link in ("in", "out", "y"):
        for s, e in enumerate(fours(LINKS[kind][link])):
            sends.setdefault(max(s - 1, 0), []).append((*parse(e), link))
    for a in (DY, X):
        for h in range(2):
            sends.setdefault(a, []).append((a, OWN[kind], 0, h, "d2d"))
    return waits, sends


def steps_of(kind, phase):
    out, slot = [], 0
    for text in TASKS[kind][phase]:
        mine, tokens = [], fours(text)
        for n, e in enumerate(tokens):
            what = 1 + "tpodx".index(e[0])
            if what <= T2P:
                q = [8 * int(f[2]) + 2 * int(f[1]) + int(f[3]) if f[0] == "t" else -1 for f in (tokens[n - 1] if n else "-", e, (tokens + ["-"])[n + 1])]
                if what == T1:
                    mine.append((T1, q[1], (q[0] >= 0) + 2 * slot + 4 * (q[2] + 1)))
                    slot = 1 - slot
                else:
                    mine.append((T2P, 8 * int(e[2]) + 2 * int(e[1]) + int(e[3]), 0))
            else:
                mine.append((what, int(e[1], 17), int(e[2], 17)))
        out.append(mine)
    return out


def table(i, values):
    out = jnp.int32(values[0])
    for n in range(1, len(values)):
        if values[n] != values[n - 1]:
            out = jnp.where(i >= n, jnp.int32(values[n]), out)
    return out


def gather_cols(src, where, q0, count, m, w, buf, s, sems):
    @pl.loop(0, count)
    def _(k):
        b, _ = where(q0 + k)
        pltpu.make_async_copy(
            src.at[pl.ds(pl.multiple_of(b * R, R), R), pl.ds(pl.multiple_of(m * w, w), w)],
            buf.at[s, pl.ds(pl.multiple_of(k * R, R), R), :], sems.at[s]).start()


def chunks(lo, hi, start, wait, work, out_start, out_wait):
    start(lo, lo % 2)

    @pl.loop(lo, hi)
    def _(m):
        s = m % 2

        @pl.when(m + 1 < hi)
        def _():
            start(m + 1, 1 - s)

        wait(s)

        @pl.when(m >= lo + 2)
        def _():
            out_wait(s)

        work(m, s)
        out_start(m, s)

    @pl.when(hi - lo >= 2)
    def _():
        out_wait(hi % 2)

    out_wait((hi - 1) % 2)


def kernel(x_ref, dy_ref, gate_ref, up_ref, wg_ref, wu_ref, wd_ref,
           part_ref, dgq_ref, dwd_ref, dyg, xg, rsb, pb, yb, accb,
           wgu, dgu, ht, out_z, acc, inc,
           ag_recv, ag_send, rs_recv, pb_recv, yb_recv, od_send, oz_send, ld, slot_in, slot_out):
    g, t = lax.axis_index("dp"), lax.axis_index("tp")
    y, z, c = t // 8, (t // 2) % 4, t % 2
    far = z // 2
    sigma, base = 1 - 2 * far, 3 * far
    corner = 1 - ((z + 1) // 2) % 2
    is_c = corner == 1
    kinds = {"C": is_c, "M": corner == 0}
    zin, zout = z + sigma, lax.rem(z - sigma + 4, 4)
    full = (dyg, xg)
    own_in = (dy_ref, x_ref)

    def dev(yy, zz, cc):
        return (g, yy * 8 + zz * 2 + cc)

    def place(p, yr):
        return y + yr * (1 - 2 * y), base + sigma * p

    def where(q):
        yy, zz = place((q % 8) // 2, q // 8)
        cr = q % 2
        return yy * 8 + zz * 2 + c + cr * (1 - 2 * c), yy * 4 + zz

    targets = {"in": dev(y, zin, c), "out": dev(y, zout, c), "y": dev(1 - y, z, c), "d2d": dev(y, z, 1 - c)}

    def half(ref, b, h):
        return ref.at[pl.ds(pl.multiple_of(b * R + h * HB, HB), HB), :]

    def block(ref, b):
        return ref.at[pl.ds(pl.multiple_of(b * R, R), R), :]

    barrier = pltpu.get_barrier_semaphore()
    for name in ("in", "y", "d2d"):
        pl.semaphore_signal(barrier, inc=1, device_id=targets[name], device_id_type=pl.DeviceIdType.MESH)

    @pl.when(corner == 0)
    def _():
        pl.semaphore_signal(barrier, inc=1, device_id=targets["out"], device_id_type=pl.DeviceIdType.MESH)

    pl.semaphore_wait(barrier, 4 - corner)

    def ag_copy(a, p, yr, h, link, own):
        yy, zz = place(p, yr)
        b = yy * 8 + zz * 2 + c
        src = own_in[a].at[pl.ds(h * HB, HB), :] if own else half(full[a], b, h)
        return pltpu.make_async_remote_copy(
            src_ref=src, dst_ref=half(full[a], b, h), send_sem=ag_send.at[a, 0 if link in ("in", "out") else 1],
            recv_sem=ag_recv.at[a, b, h], device_id=targets[link], device_id_type=pl.DeviceIdType.MESH)

    def arrived(a, b, h):
        pltpu.make_async_copy(half(full[a], b, h), half(full[a], b, h), ag_recv.at[a, b, h]).wait()

    def service(kind, waits, sends):
        for a, p, yr, h in waits:
            yy, zz = place(p, yr)
            arrived(a, yy * 8 + zz * 2 + c, h)
        for a, p, yr, h, link in sends:
            ag_copy(a, p, yr, h, link, own=(p == OWN[kind] and yr == 0)).start()

    plans = {kind: services(kind) for kind in ("C", "M")}

    def task_t1(q, code, wd, dyb, gb, ub):
        loaded, slot, after = code % 2, (code // 2) % 2, code // 4 - 1

        def loads(q, s):
            b, _ = where(q)
            return (pltpu.make_async_copy(block(dyg, b), dyb.at[s], ld.at[s]),
                    pltpu.make_async_copy(block(gate_ref, b), gb.at[s], ld.at[2 + s]),
                    pltpu.make_async_copy(block(up_ref, b), ub.at[s], ld.at[4 + s]))

        def start(q, s):
            @pl.when(q % 2 == 1)
            def _():
                for h in range(2):
                    arrived(DY, where(q)[0], h)

            for cp in loads(q, s):
                cp.start()

        @pl.when(loaded == 0)
        def _():
            start(q, slot)

        @pl.when(after >= 0)
        def _():
            start(after, 1 - slot)

        here = loads(q, slot)
        here[0].wait()
        acc[:, :C] = lax.dot_general(dyb[slot], wd[...], NT, preferred_element_type=F32)
        for cp in here[1:]:
            cp.wait()
        rc = 32

        @pl.loop(0, R // rc)
        def _(r):
            rs = pl.ds(pl.multiple_of(r * rc, rc), rc)
            to = pl.ds(pl.multiple_of(q * R + r * rc, rc), rc)
            dh, gg, uu = acc[rs, :C], gb[slot, rs, :].astype(F32), ub[slot, rs, :].astype(F32)
            s = jax.nn.sigmoid(gg)
            silu = gg * s
            acc[rs, C:2 * C] = silu * uu
            dgu[to, C:] = (dh * silu).astype(BF)
            dgu[to, :C] = ((dh * uu) * (s * (1.0 + gg * (1.0 - s)))).astype(BF)

        ht[:, pl.ds(pl.multiple_of(q * R, R), R)] = acc[:, C:2 * C].T.astype(BF)

    def product(q, n):
        lhs = dgu[pl.ds(pl.multiple_of(q * R, R), R), :]
        return lax.dot_general(lhs, wgu[pl.ds(pl.multiple_of(n * HN, HN), HN), :], NT, preferred_element_type=F32)

    def cols_of(n):
        return pl.ds(pl.multiple_of(n * HN, HN), HN)

    def od_copy(out_d, u, n):
        return pltpu.make_async_remote_copy(
            src_ref=out_d.at[n], dst_ref=pb.at[u, :, cols_of(n)], send_sem=od_send.at[n], recv_sem=pb_recv.at[u, n],
            device_id=targets["d2d"], device_id_type=pl.DeviceIdType.MESH)

    def task_t2p(q, first, out_d):
        _, u = where(q)

        @pl.loop(0, 2)
        def _(n):
            @pl.when(first == 0)
            def _():
                od_copy(out_d, u, n).wait_send()

            out_d[n] = product(q, n).astype(BF)
            od_copy(out_d, u, n).start()

    def oz_copy(j, n, u, to, dirn):
        return pltpu.make_async_remote_copy(
            src_ref=out_z.at[j % 3, n], dst_ref=rsb.at[dirn, u, :, cols_of(n)], send_sem=oz_send.at[j % 3, n],
            recv_sem=rs_recv.at[dirn, u, n], device_id=dev(y, to, c), device_id_type=pl.DeviceIdType.MESH)

    def y_copy(j, n):
        return pltpu.make_async_remote_copy(
            src_ref=out_z.at[j % 3, n], dst_ref=yb.at[:, cols_of(n)], send_sem=oz_send.at[j % 3, n],
            recv_sem=yb_recv.at[n], device_id=targets["y"], device_id_type=pl.DeviceIdType.MESH)

    def task_t2o(j, n):
        def pick(col, names):
            return jnp.where(is_c, *(table(j, [names.index(e[col]) for e in SUMS[kind]]) for kind in ("C", "M")))

        p, yr, fo, fi = (pick(col, "0123") for col in range(4))
        dest = pick(4, "IOYH")
        q = 8 * yr + 2 * p
        _, u = where(q)
        cs = cols_of(n)
        sources = (
            (jnp.int32(1), pb.at[u, :, cs], pb_recv.at[u, n]),
            (fo, rsb.at[0, u, :, cs], rs_recv.at[0, u, n]),
            (fi, rsb.at[1, u, :, cs], rs_recv.at[1, u, n]),
        )

        def fetch(s):
            flag, ref, sem = sources[s]

            @pl.when(flag == 1)
            def _():
                pltpu.make_async_copy(ref, ref, sem).wait()
                pltpu.make_async_copy(ref, inc.at[s], ld.at[s]).start()

        early = jnp.where((corner == 0) | (j >= 3) | (n == 1), 1, 0)

        @pl.when(early == 1)
        def _():
            fetch(0)

        acc[...] = product(q, n)

        @pl.when(early == 0)
        def _():
            fetch(0)

        fetch(1)
        fetch(2)
        for s, (flag, ref, sem) in enumerate(sources):
            @pl.when(flag == 1)
            def _():
                pltpu.make_async_copy(ref, inc.at[s], ld.at[s]).wait()
                acc[...] += inc[s].astype(F32)

        @pl.when(dest < HERE)
        def _():
            @pl.when(j >= 3)
            def _():
                y_copy(j, n).wait_send()

            out_z[j % 3, n] = acc[...].astype(BF)

        @pl.when(dest < Y)
        def _():
            oz_copy(j, n, u, jnp.where(dest == IN, zin, zout), jnp.where(dest == IN, 1 - corner, 1)).start()

        @pl.when(dest == Y)
        def _():
            y_copy(j, n).start()

        @pl.when(dest == HERE)
        def _():
            done = pltpu.make_async_copy(acc, part_ref.at[:, cs], ld.at[0])
            done.start()
            done.wait()

    def gather(src, q0, count, m, w, buf, s):
        gather_cols(src, where, q0, count, m, w, buf, s, slot_in)

    def task_dwd(lo, hi):
        def body(buf, out):
            def out_copy(m, s):
                return pltpu.make_async_copy(out.at[s], dwd_ref.at[:, pl.ds(pl.multiple_of(m * W, W), W)], slot_out.at[s])

            def work(m, s):
                out[s] = jnp.dot(ht[...], buf[s], preferred_element_type=F32).astype(BF)

            chunks(lo, hi, lambda m, s: gather(dyg, 0, NB, m, W, buf, s),
                   lambda s: pltpu.make_async_copy(buf.at[s], buf.at[s], slot_in.at[s]).wait(), work,
                   lambda m, s: out_copy(m, s).start(), lambda s: out_copy(0, s).wait())

        pl.run_scoped(body, pltpu.VMEM((2, NB * R, W), BF), pltpu.VMEM((2, C, W), BF))

    def x_arrived(q0, count):
        @pl.loop(0, count)
        def _(k):
            b, _ = where(q0 + 2 * k + 1)
            for h in range(2):
                arrived(X, b, h)

    def task_p1(lo, hi):
        @pl.when(lo == 0)
        def _():
            x_arrived(0, 6)

        def body(buf, out):
            def out_copy(m, s):
                return pltpu.make_async_copy(out.at[s], accb.at[pl.ds(pl.multiple_of(m * WP, WP), WP), :], slot_out.at[s])

            def work(m, s):
                out[s] = lax.dot_general(buf[s], dgu[:QA * R, :], TT, preferred_element_type=F32)

            chunks(lo, hi, lambda m, s: gather(xg, 0, QA, m, WP, buf, s),
                   lambda s: pltpu.make_async_copy(buf.at[s], buf.at[s], slot_in.at[s]).wait(), work,
                   lambda m, s: out_copy(m, s).start(), lambda s: out_copy(0, s).wait())

        pl.run_scoped(body, pltpu.VMEM((2, QA * R, WP), BF), pltpu.VMEM((2, WP, 2 * C), F32))

    def run(phase, handlers):
        steps, at = {"C": [], "M": []}, {}
        points = {kind: steps_of(kind, phase) for kind in steps}
        for n, lists in enumerate(zip(points["C"], points["M"])):
            count = max(1, *map(len, lists))
            at[n + phase * len(TASKS["C"][0])] = len(steps["C"])
            for kind, mine in zip(("C", "M"), lists):
                steps[kind] += mine + [(NONE, 0, 0)] * (count - len(mine))

        @pl.loop(0, len(steps["C"]))
        def _(i):
            for k, start in at.items():
                for kind, mine in kinds.items():
                    waits, sends = (e.get(k, []) for e in plans[kind])
                    if k and (waits or sends):
                        @pl.when((i == start) & mine)
                        def _():
                            service(kind, waits, sends)

            what, a1, a2 = (
                jnp.where(is_c, table(i, [e[col] for e in steps["C"]]), table(i, [e[col] for e in steps["M"]])) for col in range(3))
            for kind, fn in handlers.items():
                @pl.when(what == kind)
                def _():
                    fn(i, a1, a2)

    def phase_one(wd, dyb, gb, ub, out_d):
        for kind, mine in kinds.items():
            @pl.when(mine)
            def _():
                service(kind, *(e.get(0, []) for e in plans[kind]))

        weights = [
            pltpu.make_async_copy(wd_ref, wd, ld.at[3]),
            pltpu.make_async_copy(wg_ref, wgu.at[:, pl.ds(0, C)], ld.at[4]),
            pltpu.make_async_copy(wu_ref, wgu.at[:, pl.ds(C, C)], ld.at[5]),
        ]
        for cp in weights:
            cp.start()
        for a in (DY, X):
            for cp in (pltpu.make_async_copy(own_in[a], dyb.at[0], ld.at[0]), pltpu.make_async_copy(dyb.at[0], block(full[a], t), ld.at[0])):
                cp.start()
                cp.wait()
        for cp in weights:
            cp.wait()
        run(0, {
            T1: lambda i, q, code: task_t1(q, code, wd, dyb, gb, ub),
            T2P: lambda i, q, _: task_t2p(q, jnp.where(i < 3, 1, 0), out_d),
            T2O: lambda i, j, n: task_t2o(j, n),
        })
        for n in range(2):
            od_copy(out_d, 0, n).wait_send()

    pl.run_scoped(phase_one, pltpu.VMEM((C, D), BF), pltpu.VMEM((2, R, D), BF), pltpu.VMEM((2, R, C), BF), pltpu.VMEM((2, R, C), BF),
                  pltpu.VMEM((2, R, HN), BF))
    rest = pltpu.make_async_copy(dgu.at[pl.ds(QA * R, (NB - QA) * R), :], dgq_ref, ld.at[6])
    rest.start()
    run(1, {
        T2O: lambda i, j, n: task_t2o(j, n),
        DWD: lambda i, lo, hi: task_dwd(lo, hi),
        P1: lambda i, lo, hi: task_p1(lo, hi),
    })
    rest.wait()
    x_arrived(QA, (NB - QA) // 2)
    for n in range(2):
        pltpu.make_async_copy(yb.at[:, cols_of(n)], yb.at[:, cols_of(n)], yb_recv.at[n]).wait()
        for j in range(3):
            y_copy(j, n).wait_send()
    for kind, mine in kinds.items():
        @pl.when(mine)
        def _():
            sent = [e for es in plans[kind][1].values() for e in es]
            for a in (DY, X):
                for group, links in enumerate((("in", "out"), ("y", "d2d"))):
                    part = full[a].at[pl.ds(0, HB * sum(e[0] == a and e[4] in links for e in sent)), :]
                    pltpu.make_async_copy(part, part, ag_send.at[a, group]).wait()


def finish(part_ref, yb, accb, xg, dgq_ref, dwd_in, dx_ref, dwg_ref, dwu_ref, dwd_ref,
           dgq, buf, part, out, mine, theirs, done, rows, slot_in, acc_in, slot_out, ld, row_in, row_out):
    t = lax.axis_index("tp")
    y, z, c = t // 8, (t // 2) % 4, t % 2
    far = z // 2
    H = C * W // D

    def where(q):
        yr, p, cr = q // 8, (q % 8) // 2, q % 2
        return (y + yr * (1 - 2 * y)) * 8 + (3 * far + (1 - 2 * far) * p) * 2 + c + cr * (1 - 2 * c), 0

    loads = [pltpu.make_async_copy(a, b, ld.at[n]) for n, (a, b) in enumerate(((dgq_ref, dgq), (part_ref, mine), (yb, theirs)))]
    dx = pltpu.make_async_copy(done, dx_ref, ld.at[3])
    chunks = D // W

    def row(ref, m):
        return ref.at[pl.ds(pl.multiple_of(m * H, H), H), :]

    def ins(m, s):
        return (pltpu.make_async_copy(accb.at[pl.ds(pl.multiple_of(m * W, W), W), :], part.at[s], acc_in.at[s]),
                pltpu.make_async_copy(row(dwd_in, m), rows.at[m % 5], row_in.at[s]))

    def start(m):
        gather_cols(xg, where, QA, NB - QA, m, W, buf, m % 3, slot_in)
        for cp in ins(m, m % 3):
            cp.start()

    def outs(m):
        s, to = m % 2, pl.ds(pl.multiple_of(m * W, W), W)
        return (pltpu.make_async_copy(out.at[s, 0], dwg_ref.at[to, :], slot_out.at[s, 0]),
                pltpu.make_async_copy(out.at[s, 1], dwu_ref.at[to, :], slot_out.at[s, 1]),
                pltpu.make_async_copy(rows.at[m % 5], row(dwd_ref, m), row_out.at[s]))

    loads[0].start()
    for m in range(2):
        start(m)
    for cp in loads[1:]:
        cp.start()
    loads[0].wait()

    @pl.loop(0, chunks)
    def _(m):
        s = m % 3

        @pl.when(m + 2 < chunks)
        def _():
            start(m + 2)

        pltpu.make_async_copy(buf.at[s], buf.at[s], slot_in.at[s]).wait()
        for cp in ins(m, s):
            cp.wait()

        @pl.when(m >= 2)
        def _():
            for cp in outs(m - 2):
                cp.wait()

        total = part[s] + lax.dot_general(buf[s], dgq[...], TT, preferred_element_type=F32)
        out[m % 2, 0] = total[:, :C].astype(BF)
        out[m % 2, 1] = total[:, C:].astype(BF)
        for cp in outs(m):
            cp.start()

        @pl.when(m == 2)
        def _():
            for cp in loads[1:]:
                cp.wait()
            done[...] = (mine[...] + theirs[...].astype(F32)).astype(BF)
            dx.start()

    for m in range(2):
        for cp in outs(chunks - 2 + m):
            cp.wait()
    dx.wait()


def solution(mesh):
    def step(x, dy, gate, up, w_gate, w_up, w_down):
        hbm = pl.BlockSpec(memory_space=pl.ANY)
        S = jax.ShapeDtypeStruct
        dma = pltpu.SemaphoreType.DMA
        part, dgq, dwd, _, xg, _, _, yb, accb = pl.pallas_call(
            kernel,
            out_shape=[
                S((R, D), F32), S(((NB - QA) * R, 2 * C), BF), S((C, D), BF),
                S((NB * R, D), BF), S((NB * R, D), BF), S((2, 8, R, D), BF), S((8, R, D), BF), S((R, D), BF),
                S((D, 2 * C), F32),
            ],
            in_specs=[hbm] * 7,
            out_specs=[hbm] * 9,
            scratch_shapes=[
                pltpu.VMEM((D, 2 * C), BF),
                pltpu.VMEM((NB * R, 2 * C), BF),
                pltpu.VMEM((C, NB * R), BF),
                pltpu.VMEM((3, 2, R, HN), BF),
                pltpu.VMEM((R, HN), F32),
                pltpu.VMEM((3, R, HN), BF),
                dma((2, NB, 2)), dma((2, 2)), dma((2, 8, 2)), dma((8, 2)), dma((2,)), dma((2,)), dma((3, 2)), dma((7,)), dma((2,)),
                dma((2,)),
            ],
            compiler_params=pltpu.CompilerParams(collective_id=0, has_side_effects=True, vmem_limit_bytes=LIMIT),
            name="gather_and_sum",
        )(x, dy, gate, up, w_gate, w_up, w_down)
        return pl.pallas_call(
            finish,
            out_shape=[S((R, D), BF), S((D, C), BF), S((D, C), BF), S((C, D), BF)],
            in_specs=[hbm] * 6,
            out_specs=[hbm] * 4,
            scratch_shapes=[
                pltpu.VMEM(((NB - QA) * R, 2 * C), BF),
                pltpu.VMEM((3, (NB - QA) * R, W), BF),
                pltpu.VMEM((3, W, 2 * C), F32),
                pltpu.VMEM((2, 2, W, C), BF),
                pltpu.VMEM((R, D), F32),
                pltpu.VMEM((R, D), BF),
                pltpu.VMEM((R, D), BF),
                pltpu.VMEM((5, C * W // D, D), BF),
                dma((3,)), dma((3,)), dma((2, 2)), dma((4,)), dma((3,)), dma((2,)),
            ],
            compiler_params=pltpu.CompilerParams(vmem_limit_bytes=LIMIT),
            name="finish",
        )(part, yb, accb, xg, dgq, dwd)

    rows, cols = P(("dp", "tp"), None), P("dp", "tp")
    return jax.shard_map(
        step,
        mesh=mesh,
        in_specs=(rows, rows, cols, cols, P(None, "tp"), P(None, "tp"), P("tp", None)),
        out_specs=(rows, cols, cols, rows),
        check_vma=False,
    )
```

time: 1040 us -> 434 us (0.42)
  waiting for transfers between devices: 554 us -> 0 us
  Pallas kernels: 0 us -> 427 us
  matrix products: 327 us -> 0 us
  local copies, waits for them, and re-layouts: 56.9 us -> 0 us
  starting transfers between devices: 47.5 us -> 0 us
  other arithmetic: 26.2 us -> 0 us
  between operations: 14.3 us -> 0.8 us
    pallas_call x0 -> x2, Pallas kernels: none -> 427 us  [the longest x1 400 us: step(): pl.pallas_call(kernel, out_shape=[S((R, D), F32), S(((NB - QA) * R, 2 * C...]
    dot_general x17 -> x0, waiting for transfers between devices: 353 us -> none  [by_group(): jnp.einsum('gta,gtb->gab', a, b, preferred_element_type=jnp.float32)]
    dot_general x13 -> x0, matrix products: 327 us -> none  [the longest x10 197 us: by_group(): jnp.einsum('gta,gtb->gab', a, b, preferred_element_type=jnp.float32)]
    unnamed x5 -> x0, waiting for transfers between devices: 171 us -> none
    dot_general x17 -> x0, starting transfers between devices: 47.4 us -> none  [by_group(): jnp.einsum('gta,gtb->gab', a, b, preferred_element_type=jnp.float32)]
    unnamed x6 -> x0, local copies, waits for them, and re-layouts: 35.5 us -> none
    reshape x1 -> x0, waiting for transfers between devices: 30.1 us -> none  [by_group(): a, b = (t.reshape(groups, -1, t.shape[-1]) for t in (a, b))]
    reshape x2 -> x0, other arithmetic: 26.2 us -> none  [the longest x1 16.9 us: by_group(): a, b = (t.reshape(groups, -1, t.shape[-1]) for t in (a, b))]
  transfers between devices with their start and end apart: 20 -> 0, of which waited for: 17 -> 0; matrix products, arithmetic and copies ran while one was open for 39% -> 0% of each run, Pallas kernels for 0% -> 0%
where the time goes in v1:
time: 434 us; the launch traced here: 428 us
  Pallas kernels  427 us (98%)
    pallas_call x1, Pallas kernels, step(): pl.pallas_call(kernel, out_shape=[S((R, D), F32), S(((NB - QA) * R, 2 * C...  400 us
    pallas_call x1, Pallas kernels, step(): pl.pallas_call(finish, out_shape=[S((R, D), BF), S((D, C), BF), S((D, C),...  27.6 us

profile of v1, /device:TPU:0, one launch (start us, length us, event | category | flops | bytes accessed | tf_op | source)
XLA Modules:
  0.0 427.9 jit_solution(12729588034489416007)
XLA Ops:
  0.6 399.5 %gather_and_sum.1 = (f32[256,4096]{1,0:T(8,128)}, bf16[1024,1792]{1,0:T(8,128)(2,1)}, bf16[896,4096]{1,0:T(8,128)(2,1)}, bf16[4096,4096]{1,0:T(8,128)(2,1)}, bf1...) custom-call(bf16[256,4096]{1,0:T(8,128)(2,1)} %x_ref.1, ...), custom_call_target="tpu_custom_call" | custom-call | tf_op jit(solution)/shard_map/gather_and_sum/pallas_call | solution.py:554
  400.2 27.6 %finish.1 = (bf16[256,4096]{1,0:T(8,128)(2,1)}, bf16[4096,896]{1,0:T(8,128)(2,1)}, bf16[4096,896]{1,0:T(8,128)(2,1)}, bf16[896,4096]{1,0:T(8,128)(2,1)}) custom-call(f32[256,4096]{1,0:T(8,128)} %get-tuple-element.10.part_ref, bf16[256,4096]{1,0:T(8,128)(2,1)} %get-tuple-element.11.yb, f32[4096,1792]{1,0:T(8,128)} %get-tuple-element.12.accb, ...), custom_call_target="tpu_custom_call" | custom-call | tf_op jit(solution)/shard_map/finish/pallas_call | solution.py:576

commit v2 on v1

--- a/solution.py
+++ b/solution.py
@@ -11,6 +11,7 @@
 HB, HN = R // 2, D // 2
 NB = 16
 W, WP = 512, 256
+DE = 2560
 QA = 12
 NT, TT = (((1,), (1,)), ((), ())), (((0,), (0,)), ((), ()))
 DY, X = 0, 1
@@ -28,17 +29,17 @@
     },
 }
 OWN = {"C": 0, "M": 1}
-NONE, T1, T2P, T2O, DWD, P1 = range(6)
+NONE, T1, T2P, T2O, DWD, P1, P3 = range(7)
 TASKS = {
     "C": (
         ("t000t001p001", "", "t100t010t101t011", "p101p011", "t110t111p111o00-o01-", "t200t201p201", "t300t301p301o10-o11-",
          "t210t211p211", "t310t311p311o20-o21-"),
-        ("d03-", "o30-o31-d35-", "d58-", "o40-o41-", "x04-", "o50-o51-x48-o60-", "o61-x8c-", "xcg-", "o70-o71-"),
+        ("d03-", "o30-o31-d35-", "d58-", "o40-o41-", "x04-", "o50-o51-x48-o60-", "o61-x8a-zac-", "zcg-", "o70-o71-"),
     ),
     "M": (
         ("t100t101p101", "", "t000t200t110t001", "t201t111p001", "t300t010t301t011", "p301p201p111", "t210t211p211p011", "",
          "t310t311p311o00-"),
-        ("o01-d02-", "d24-o10-", "o11-d46-", "o20-o30-d68-", "o21-o31-x04-", "o40-o60-x48-o50-", "o41-o61-o51-x8c-", "xcg-", "o70-o71-"),
+        ("o01-d03-", "d35-o10-", "o11-d58-", "o20-o30-x03-", "o21-o31-x37-", "o40-o60-o50-x7a-", "o41-o61-o51-zac-", "zcg-", "o70-o71-"),
     ),
 }
 IN, OUT, Y, HERE = range(4)
@@ -83,7 +84,7 @@
     for text in TASKS[kind][phase]:
         mine, tokens = [], fours(text)
         for n, e in enumerate(tokens):
-            what = 1 + "tpodx".index(e[0])
+            what = 1 + "tpodxz".index(e[0])
             if what <= T2P:
                 q = [8 * int(f[2]) + 2 * int(f[1]) + int(f[3]) if f[0] == "t" else -1 for f in (tokens[n - 1] if n else "-", e, (tokens + ["-"])[n + 1])]
                 if what == T1:
@@ -142,7 +143,7 @@
 
 
 def kernel(x_ref, dy_ref, gate_ref, up_ref, wg_ref, wu_ref, wd_ref,
-           part_ref, dgq_ref, dwd_ref, dyg, xg, rsb, pb, yb, accb,
+           part_ref, dgq_ref, dwd_ref, late_ref, dyg, xg, rsb, pb, yb, accb,
            wgu, dgu, ht, out_z, acc, inc,
            ag_recv, ag_send, rs_recv, pb_recv, yb_recv, od_send, oz_send, ld, slot_in, slot_out):
     g, t = lax.axis_index("dp"), lax.axis_index("tp")
@@ -391,6 +392,24 @@
                    lambda m, s: out_copy(m, s).start(), lambda s: out_copy(0, s).wait())
 
         pl.run_scoped(body, pltpu.VMEM((2, QA * R, WP), BF), pltpu.VMEM((2, WP, 2 * C), F32))
+
+    def task_p3(lo, hi):
+        @pl.when(lo == DE // WP)
+        def _():
+            x_arrived(QA, (NB - QA) // 2)
+
+        def body(buf, out):
+            def out_copy(m, s):
+                return pltpu.make_async_copy(out.at[s], late_ref.at[pl.ds(pl.multiple_of(m * WP - DE, WP), WP), :], slot_out.at[s])
+
+            def work(m, s):
+                out[s] = lax.dot_general(buf[s], dgu[...], TT, preferred_element_type=F32).astype(BF)
+
+            chunks(lo, hi, lambda m, s: gather(xg, 0, NB, m, WP, buf, s),
+                   lambda s: pltpu.make_async_copy(buf.at[s], buf.at[s], slot_in.at[s]).wait(), work,
+                   lambda m, s: out_copy(m, s).start(), lambda s: out_copy(DE // WP, s).wait())
+
+        pl.run_scoped(body, pltpu.VMEM((2, NB * R, WP), BF), pltpu.VMEM((2, WP, 2 * C), BF))
 
     def run(phase, handlers):
         steps, at = {"C": [], "M": []}, {}
@@ -453,9 +472,9 @@
         T2O: lambda i, j, n: task_t2o(j, n),
         DWD: lambda i, lo, hi: task_dwd(lo, hi),
         P1: lambda i, lo, hi: task_p1(lo, hi),
+        P3: lambda i, lo, hi: task_p3(lo, hi),
     })
     rest.wait()
-    x_arrived(QA, (NB - QA) // 2)
     for n in range(2):
         pltpu.make_async_copy(yb.at[:, cols_of(n)], yb.at[:, cols_of(n)], yb_recv.at[n]).wait()
         for j in range(3):
@@ -470,38 +489,34 @@
                     pltpu.make_async_copy(part, part, ag_send.at[a, group]).wait()
 
 
-def finish(part_ref, yb, accb, xg, dgq_ref, dwd_in, dx_ref, dwg_ref, dwu_ref, dwd_ref,
-           dgq, buf, part, out, mine, theirs, done, rows, slot_in, acc_in, slot_out, ld, row_in, row_out):
+def finish(part_ref, yb, accb, xg, dgq_ref, dwd_in, late_ref, dx_ref, dwg_ref, dwu_ref, dwd_ref,
+           dgq, buf, part, out, mine, theirs, done, late, down, slot_in, acc_in, slot_out, ld, st):
     t = lax.axis_index("tp")
     y, z, c = t // 8, (t // 2) % 4, t % 2
     far = z // 2
-    H = C * W // D
 
     def where(q):
         yr, p, cr = q // 8, (q % 8) // 2, q % 2
         return (y + yr * (1 - 2 * y)) * 8 + (3 * far + (1 - 2 * far) * p) * 2 + c + cr * (1 - 2 * c), 0
 
-    loads = [pltpu.make_async_copy(a, b, ld.at[n]) for n, (a, b) in enumerate(((dgq_ref, dgq), (part_ref, mine), (yb, theirs)))]
-    dx = pltpu.make_async_copy(done, dx_ref, ld.at[3])
-    chunks = D // W
-
-    def row(ref, m):
-        return ref.at[pl.ds(pl.multiple_of(m * H, H), H), :]
-
-    def ins(m, s):
-        return (pltpu.make_async_copy(accb.at[pl.ds(pl.multiple_of(m * W, W), W), :], part.at[s], acc_in.at[s]),
-                pltpu.make_async_copy(row(dwd_in, m), rows.at[m % 5], row_in.at[s]))
+    pairs = ((dgq_ref, dgq), (late_ref, late), (dwd_in, down), (part_ref, mine), (yb, theirs))
+    loads = [pltpu.make_async_copy(a, b, ld.at[n]) for n, (a, b) in enumerate(pairs)]
+    tail = pl.ds(DE, D - DE)
+    pairs = ((late.at[:, pl.ds(0, C)], dwg_ref.at[tail, :]), (late.at[:, pl.ds(C, C)], dwu_ref.at[tail, :]), (down, dwd_ref), (done, dx_ref))
+    stores = [pltpu.make_async_copy(a, b, st.at[n]) for n, (a, b) in enumerate(pairs)]
+    count = DE // W
+
+    def acc_copy(m):
+        return pltpu.make_async_copy(accb.at[pl.ds(pl.multiple_of(m * W, W), W), :], part.at[m % 3], acc_in.at[m % 3])
 
     def start(m):
         gather_cols(xg, where, QA, NB - QA, m, W, buf, m % 3, slot_in)
-        for cp in ins(m, m % 3):
-            cp.start()
+        acc_copy(m).start()
 
     def outs(m):
         s, to = m % 2, pl.ds(pl.multiple_of(m * W, W), W)
         return (pltpu.make_async_copy(out.at[s, 0], dwg_ref.at[to, :], slot_out.at[s, 0]),
-                pltpu.make_async_copy(out.at[s, 1], dwu_ref.at[to, :], slot_out.at[s, 1]),
-                pltpu.make_async_copy(rows.at[m % 5], row(dwd_ref, m), row_out.at[s]))
+                pltpu.make_async_copy(out.at[s, 1], dwu_ref.at[to, :], slot_out.at[s, 1]))
 
     loads[0].start()
     for m in range(2):
@@ -510,17 +525,16 @@
         cp.start()
     loads[0].wait()
 
-    @pl.loop(0, chunks)
+    @pl.loop(0, count)
     def _(m):
         s = m % 3
 
-        @pl.when(m + 2 < chunks)
+        @pl.when(m + 2 < count)
         def _():
             start(m + 2)
 
         pltpu.make_async_copy(buf.at[s], buf.at[s], slot_in.at[s]).wait()
-        for cp in ins(m, s):
-            cp.wait()
+        acc_copy(m).wait()
 
         @pl.when(m >= 2)
         def _():
@@ -533,17 +547,29 @@
         for cp in outs(m):
             cp.start()
 
+        @pl.when(m == 0)
+        def _():
+            loads[1].wait()
+            for cp in stores[:2]:
+                cp.start()
+
+        @pl.when(m == 1)
+        def _():
+            loads[2].wait()
+            stores[2].start()
+
         @pl.when(m == 2)
         def _():
-            for cp in loads[1:]:
+            for cp in loads[3:]:
                 cp.wait()
             done[...] = (mine[...] + theirs[...].astype(F32)).astype(BF)
-            dx.start()
+            stores[3].start()
 
     for m in range(2):
-        for cp in outs(chunks - 2 + m):
+        for cp in outs(count - 2 + m):
             cp.wait()
-    dx.wait()
+    for cp in stores:
+        cp.wait()
 
 
 def solution(mesh):
@@ -551,15 +577,15 @@
         hbm = pl.BlockSpec(memory_space=pl.ANY)
         S = jax.ShapeDtypeStruct
         dma = pltpu.SemaphoreType.DMA
-        part, dgq, dwd, _, xg, _, _, yb, accb = pl.pallas_call(
+        part, dgq, dwd, late, _, xg, _, _, yb, accb = pl.pallas_call(
             kernel,
             out_shape=[
-                S((R, D), F32), S(((NB - QA) * R, 2 * C), BF), S((C, D), BF),
+                S((R, D), F32), S(((NB - QA) * R, 2 * C), BF), S((C, D), BF), S((D - DE, 2 * C), BF),
                 S((NB * R, D), BF), S((NB * R, D), BF), S((2, 8, R, D), BF), S((8, R, D), BF), S((R, D), BF),
-                S((D, 2 * C), F32),
+                S((DE, 2 * C), F32),
             ],
             in_specs=[hbm] * 7,
-            out_specs=[hbm] * 9,
+            out_specs=[hbm] * 10,
             scratch_shapes=[
                 pltpu.VMEM((D, 2 * C), BF),
                 pltpu.VMEM((NB * R, 2 * C), BF),
@@ -576,7 +602,7 @@
         return pl.pallas_call(
             finish,
             out_shape=[S((R, D), BF), S((D, C), BF), S((D, C), BF), S((C, D), BF)],
-            in_specs=[hbm] * 6,
+            in_specs=[hbm] * 7,
             out_specs=[hbm] * 4,
             scratch_shapes=[
                 pltpu.VMEM(((NB - QA) * R, 2 * C), BF),
@@ -586,12 +612,13 @@
                 pltpu.VMEM((R, D), F32),
                 pltpu.VMEM((R, D), BF),
                 pltpu.VMEM((R, D), BF),
-                pltpu.VMEM((5, C * W // D, D), BF),
-                dma((3,)), dma((3,)), dma((2, 2)), dma((4,)), dma((3,)), dma((2,)),
+                pltpu.VMEM((D - DE, 2 * C), BF),
+                pltpu.VMEM((C, D), BF),
+                dma((3,)), dma((3,)), dma((2, 2)), dma((5,)), dma((4,)),
             ],
             compiler_params=pltpu.CompilerParams(vmem_limit_bytes=LIMIT),
             name="finish",
-        )(part, yb, accb, xg, dgq, dwd)
+        )(part, yb, accb, xg, dgq, dwd, late)
 
     rows, cols = P(("dp", "tp"), None), P("dp", "tp")
     return jax.shard_map(

time: 434 us -> 428 us (0.986); the launches traced: 428 us -> 427 us
  no operation moved by 1% of the time
where the time goes in v2:
time: 428 us; the launch traced here: 427 us
  Pallas kernels  426 us (100%)
    pallas_call x1, Pallas kernels, step(): pl.pallas_call(kernel, out_shape=[S((R, D), F32), S(((NB - QA) * R, 2 * C...  401 us
    pallas_call x1, Pallas kernels, step(): pl.pallas_call(finish, out_shape=[S((R, D), BF), S((D, C), BF), S((D, C),...  25.3 us

profile of v2, /device:TPU:0, one launch (start us, length us, event | category | flops | bytes accessed | tf_op | source)
XLA Modules:
  0.0 426.8 jit_solution(11091413451434120873)
XLA Ops:
  0.6 400.7 %gather_and_sum.1 = (f32[256,4096]{1,0:T(8,128)}, bf16[1024,1792]{1,0:T(8,128)(2,1)}, bf16[896,4096]{1,0:T(8,128)(2,1)}, bf16[1536,1792]{1,0:T(8,128)(2,1)}, bf1...) custom-call(bf16[256,4096]{1,0:T(8,128)(2,1)} %x_ref.1, ...), custom_call_target="tpu_custom_call" | custom-call | tf_op jit(solution)/shard_map/gather_and_sum/pallas_call | solution.py:580
  401.4 25.3 %finish.1 = (bf16[256,4096]{1,0:T(8,128)(2,1)}, bf16[4096,896]{1,0:T(8,128)(2,1)}, bf16[4096,896]{1,0:T(8,128)(2,1)}, bf16[896,4096]{1,0:T(8,128)(2,1)}) custom-call(f32[256,4096]{1,0:T(8,128)} %get-tuple-element.11.part_ref, bf16[256,4096]{1,0:T(8,128)(2,1)} %get-tuple-element.12.yb, f32[2560,1792]{1,0:T(8,128)} %get-tuple-element.13.accb, ...), custom_call_target="tpu_custom_call" | custom-call | tf_op jit(solution)/shard_map/finish/pallas_call | solution.py:602
